TPU v7x, 32 devices: a whole 2x2x4 slice. The times are simulated.
32 devices in a mesh: frame: 4 (over z), space: 8 (over y, x, core).
Axes of the slice: x: 2, y: 2, z: 4, core: 2. Of those that a mesh axis runs over, the one named last changes fastest.
Arguments:
- tokens: bfloat16 [32, 152, 1024], P('space', 'frame'), may hold values from -16 to 16
- tube_count: int32 [8], P('space'), may hold values from 1 to 4, as said below
- ln_gain: float32 [1024], replicated, may hold values from 0.25 to 1.75
- ln_bias: float32 [1024], replicated, may hold values from -3 to 3
- w_qkv: bfloat16 [1024, 1536], replicated, may hold values from -1.5 to 1.5
- w_out: bfloat16 [512, 1024], replicated, may hold values from -0.25 to 0.25
Outputs:
- mixed: bfloat16 [32, 152, 1024], P('space', 'frame')
Inputs may be any that keep to these rules, and one draw needn't show every extreme that they name: tube_count[s] is how many of the 4 slots of space index s hold visible tubes; they are the first ones. Some index has all 4, some only 1.
All inputs are finite; a program needn't handle non-finite values.
Results may differ from a plain program's by a relative error of at most 0.005.
Values may be sent and summed in bfloat16 or wider, within the bound.
No kernel may reach another device: no remote copies, remote signals or barrier semaphores. Data moves between devices by JAX's collectives and lax.ppermute only.
A program may use at most 128 MiB of HBM per device.

v0:
```python
import jax
import jax.numpy as jnp
from jax import lax
from jax.sharding import PartitionSpec as P

HEADS = 8
EPSILON = 1e-06
NEG_FILL = -1e30


def layer_norm(flat, ln_gain, ln_bias):
    values32 = flat.astype(jnp.float32)
    center = values32 - jnp.mean(values32, axis=-1, keepdims=True)
    spread = jnp.mean(center * center, axis=-1, keepdims=True)
    return (center * lax.rsqrt(spread + EPSILON) * ln_gain + ln_bias).astype(jnp.bfloat16)


def live_mask(counts, slots_dev, time_dev):
    slot_ids = jnp.arange(slots_dev)[None, :, None]
    marks = jnp.broadcast_to(
        slot_ids < counts[:, None, None], (counts.shape[0], slots_dev, time_dev)
    )
    return marks.reshape(-1)


def attend(carry, query_heads, key_block, value_block, live_keys, scaling):
    best_now, total_now, accum = carry
    heads = query_heads.shape[1]
    key_heads = key_block.reshape(key_block.shape[0], heads, -1)
    value_heads = value_block.reshape(value_block.shape[0], heads, -1)
    scores = (
        jnp.einsum("qhd,khd->hqk", query_heads, key_heads, preferred_element_type=jnp.float32)
        * scaling
    )
    scores = jnp.where(live_keys[None, None, :], scores, NEG_FILL)
    best_next = jnp.maximum(best_now, jnp.max(scores, axis=-1))
    fading = jnp.exp(best_now - best_next)
    weights = jnp.exp(scores - best_next[..., None])
    total_next = total_now * fading + jnp.sum(weights, axis=-1)
    accum = accum * fading[..., None] + jnp.einsum(
        "hqk,khd->hqd",
        weights.astype(jnp.bfloat16),
        value_heads,
        preferred_element_type=jnp.float32,
    )
    return (best_next, total_next, accum)


def make_fold(query_heads, vis_dev, time_dev, scaling):
    rows_dev = vis_dev * time_dev

    def fold_masked(carry, piece, start):
        key_all, value_all, count_all = piece
        width_in = key_all.shape[1]
        shards = count_all.shape[0]
        group = 1
        for unused_bit in range(6):
            if shards % (group * 2) == 0 and group * rows_dev < 2048:
                group = group * 2
        blocks = shards // group
        key_groups = key_all.reshape(blocks, group * rows_dev, width_in)
        value_groups = value_all.reshape(blocks, group * rows_dev, width_in)
        count_groups = count_all.reshape(blocks, group)

        def step_group(state, item):
            key_group, value_group, count_group = item
            marks = live_mask(count_group, vis_dev, time_dev)
            return (attend(state, query_heads, key_group, value_group, marks, scaling), None)

        carry, unused = lax.scan(step_group, carry, (key_groups, value_groups, count_groups))
        return carry

    return fold_masked


def start_state(heads, rows, head_size):
    return (
        jnp.full((heads, rows), NEG_FILL, jnp.float32),
        jnp.zeros((heads, rows), jnp.float32),
        jnp.zeros((heads, rows, head_size), jnp.float32),
    )


def on_device(tokens, tube_count, ln_gain, ln_bias, w_qkv, w_out):
    vis_dev, time_dev, width = tokens.shape
    rows_dev = vis_dev * time_dev
    inner = w_out.shape[0]
    head_size = inner // HEADS
    flat = tokens.reshape(rows_dev, width)
    normed = layer_norm(flat, ln_gain, ln_bias)
    projected = jnp.dot(normed, w_qkv, preferred_element_type=jnp.float32).astype(jnp.bfloat16)
    scaling = head_size ** (-0.5)
    frames = lax.axis_size("frame")
    local_heads = HEADS // frames
    stacked = projected.reshape(rows_dev, 3, HEADS, head_size)
    regrouped = lax.all_to_all(stacked, "frame", split_axis=2, concat_axis=0, tiled=True)
    all_rows = regrouped.shape[0]
    query_local = regrouped[:, 0]
    key_local = regrouped[:, 1].reshape(all_rows, local_heads * head_size)
    value_local = regrouped[:, 2].reshape(all_rows, local_heads * head_size)
    counts_rep = jnp.tile(tube_count, frames)
    fold_fn = make_fold(query_local, vis_dev, time_dev, scaling)
    state = fold_fn(
        start_state(local_heads, all_rows, head_size),
        (
            lax.all_gather(key_local, "space", axis=0, tiled=True),
            lax.all_gather(value_local, "space", axis=0, tiled=True),
            lax.all_gather(counts_rep, "space", axis=0, tiled=True),
        ),
        jnp.int32(0),
    )
    best_final, total_final, accum_final = state
    attended = (accum_final / total_final[..., None]).astype(jnp.bfloat16)
    attended = jnp.transpose(attended, (1, 0, 2))
    returned = lax.all_to_all(attended, "frame", split_axis=0, concat_axis=1, tiled=True)
    attended = returned.reshape(rows_dev, inner)
    mixed = flat.astype(jnp.float32) + jnp.dot(attended, w_out, preferred_element_type=jnp.float32)
    own_live = live_mask(tube_count, vis_dev, time_dev)
    mixed = jnp.where(own_live[:, None], mixed, 0.0)
    return mixed.astype(jnp.bfloat16).reshape(vis_dev, time_dev, width)


def solution(mesh):
    in_specs = (P("space", "frame", None), P("space"), P(), P(), P(), P())
    out_specs = P("space", "frame", None)
    return jax.shard_map(
        on_device, mesh=mesh, in_specs=in_specs, out_specs=out_specs, check_vma=False
    )
```

profile of v0, /device:TPU:0, one launch (start us, length us, event | category | flops | bytes accessed | tf_op | source)
XLA Modules:
  0.0 166.7 jit_solution(1666170860876456033)
XLA Ops:
  6.5 1.3 convert_reduce_fusion
  8.0 1.3 multiply_reduce_fusion
  9.3 1.9 %copy.42 = f32[4,38,1024]{2,1,0:T(8,128)} copy(bf16[4,38,1024]{2,0,1:T(4,128)(2,1)} %param.8) | data formatting | bytes 933888 | tf_op jit(solution)/shard_map/convert_element_type | solution.py:117
  11.4 2.0 %reshape.120 = f32[152,1024]{1,0:T(8,128)} reshape(f32[4,38,1024]{2,1,0:T(8,128)} %copy.42) | data formatting | bytes 1245184 | tf_op jit(solution)/shard_map/convert_element_type | solution.py:117
  13.4 2.6 %convolution_convert_fusion = bf16[152,1536]{1,0:T(8,128)(2,1)} fusion(bf16[1024,1536]{1,0:T(8,128)(2,1)S(1)} %copy-done, f32[152,1024]{1,0:T(8,128)} %reshape.120, f32[1024]{0:T(1024)} %param.11, f32[1024]{0:T(1024)} %param.10, f32[152]{0:T(256)S(1)} %rsqrt.12, f32[152]{0:T(256)S(1)} %div.17), kind=kOutput, calls=%fused_computation.22 | convolution fusion | flops 479162368 | bytes 4244672 | tf_op jit(solution)/shard_map/dot_general | solution.py:91
  16.1 2.4 %reshape.115 = bf16[152,3,8,64]{3,2,1,0:T(8,128)(2,1)} reshape(bf16[152,1536]{1,0:T(8,128)(2,1)} %convolution_convert_fusion) | data formatting | bytes 933888 | tf_op jit(solution)/shard_map/reshape | solution.py:95
  18.4 2.8 %copy.46 = bf16[152,3,8,64]{0,3,1,2:T(8,128)(2,1)} copy(bf16[152,3,8,64]{3,2,1,0:T(8,128)(2,1)} %reshape.115) | data formatting | bytes 933888 | tf_op jit(solution)/shard_map/reshape | solution.py:95
  21.3 26.5 %all_to_all.33 = bf16[152,3,8,64]{0,3,1,2:T(8,128)(2,1)S(1)} all-to-all(bf16[152,3,8,64]{0,3,1,2:T(8,128)(2,1)} %copy.46), channel_id=1, replica_groups=mesh['frame'=4,'space'=8] {'frame'}, dimensions={2} | all-to-all | bytes 933888 | tf_op jit(solution)/shard_map/all_to_all | solution.py:96
  47.7 1.5 copy.47
  49.2 2.7 %all_to_all.27 = bf16[608,3,2,64]{0,3,2,1:T(8,128)(2,1)} reshape(bf16[4,152,3,2,64]{1,0,4,3,2:T(4,128)(2,1)} %copy.47) | data formatting | bytes 933888 | tf_op jit(solution)/shard_map/all_to_all | solution.py:96
  51.9 1.8 %fusion.20 = (bf16[608,1,2,64]{0,3,2,1:T(8,128)(2,1)}, bf16[608,2,64]{0,2,1:T(8,128)(2,1)S(1)}, bf16[608,1,2,64]{0,3,2,1:T(8,128)(2,1)S(1)}) fusion(bf16[608,3,2,64]{0,3,2,1:T(8,128)(2,1)} %all_to_all.27), kind=kLoop, calls=%fused_computation.40 | loop fusion | bytes 933888 | tf_op jit(solution)/shard_map/slice | solution.py:100
  53.7 1.7 %copy.49 = bf16[608,128]{1,0:T(8,128)(2,1)} copy(bf16[608,128]{0,1:T(8,128)(2,1)} %bitcast.69) | data formatting | bytes 311296 | tf_op jit(solution)/shard_map/reshape;squeeze | solution.py:100
  58.3 8.1 %all-reduce = s32[32]{0:T(128)S(1)} all-reduce(s32[32]{0:T(128)S(1)} %broadcast_dynamic-update-slice_fusion), channel_id=1, replica_groups=mesh['frame'=4,'space'=8] {'space'}, use_global_device_ids=true, to_apply=%add | all-reduce | flops 32 | bytes 256
  66.5 12.4 %all-gather.5.cloned.1.call-done = bf16[4864,128]{1,0:T(8,128)(2,1)} async-done(((bf16[608,128]{1,0:T(8,128)(2,1)}), bf16[4864,128]{1,0:T(8,128)(2,1)}) %all-gather.5.cloned.1.call-update) | async-done | bytes 1245200 | tf_op jit(solution)/shard_map/all_gather | solution.py:107
  78.8 26.1 %all-gather.3.cloned.1.call-done = bf16[4864,128]{1,0:T(8,128)(2,1)} async-done(((bf16[608,128]{1,0:T(8,128)(2,1)}), bf16[4864,128]{1,0:T(8,128)(2,1)}) %all-gather.3.cloned.1.call-update) | async-done | bytes 1245200 | tf_op jit(solution)/shard_map/all_gather | solution.py:106
  105.0 32.1 %while.15 = (s32[]{:T(128)}, f32[2,608]{1,0:T(2,128)S(1)}, f32[2,608]{1,0:T(2,128)S(1)}, f32[2,608,64]{1,2,0:T(8,128)}, s32[2,16]{1,0:T(2,128)S(1)}, /*index=5*/...) while((s32[]{:T(128)}, f32[2,608]{1,0:T(2,128)S(1)}, ...), condition=%wide.region_5.6_spmd.clone, body=%wide.region_2.5_spmd.clone.sunk | while | flops 789841920 | bytes 47565588 | solution.py:70
  105.3 2.4 %constant_dynamic-slice_fusion.4 = (bf16[1,2432,128]{2,1,0:T(8,128)(2,1)}, bf16[1,2432,128]{2,1,0:T(8,128)(2,1)}) fusion(bf16[2,2432,128]{2,1,0:T(8,128)(2,1)} %get-tuple-element.222, s32[]{:T(128)S(6)} %copy.73, bf16[2,2432,128]{2,1,0:T(8,128)(2,1)} %get-tuple-element.220), kind=kLoop, calls=%fused_computation.16.clone.1 | loop fusion | bytes 2490372 | tf_op jit(solution)/shard_map/while/body/jit(dynamic_index_in_dim)/dynamic_slice | solution.py:70
  107.7 2.1 %copy.66 = bf16[1,2432,128]{1,2,0:T(8,128)(2,1)} copy(bf16[1,2432,128]{2,1,0:T(8,128)(2,1)} %get-tuple-element.189) | data formatting | bytes 1245184 | tf_op jit(solution)/shard_map/while/body/jit(dynamic_index_in_dim)/dynamic_slice | solution.py:70
  109.8 2.1 %copy.67 = bf16[1,2432,128]{1,2,0:T(8,128)(2,1)} copy(bf16[1,2432,128]{2,1,0:T(8,128)(2,1)} %get-tuple-element.193) | data formatting | bytes 1245184 | tf_op jit(solution)/shard_map/while/body/jit(dynamic_index_in_dim)/dynamic_slice | solution.py:70
  111.9 3.1 %bitcast_reduce_fusion.2 = (f32[2,608]{1,0:T(2,128)S(1)}, f32[2,2432,608]{1,2,0:T(8,128)S(1)}) fusion(pred[2432]{0:T(1024)(128)(4,1)S(1)} %broadcast_in_dim.100, bf16[2432,2,64]{0,2,1:T(8,128)(2,1)} %bitcast.60, bf16[608,2,64]{0,2,1:T(8,128)(2,1)S(1)} %get-tuple-element.221), kind=kOutput, calls=%fused_computation.1.clone.1 | convolution fusion | flops 387406656 | bytes 12614784 | tf_op jit(solution)/shard_map/while/body/eval_jaxpr/qhd,khd->hqk/dot_general | solution.py:32
  115.1 2.5 %fusion.42 = f32[2,608]{1,0:T(2,128)S(1)} fusion(f32[2,2432,608]{1,2,0:T(8,128)S(1)} %get-tuple-element.191, f32[2,608]{1,0:T(2,128)S(1)} %fusion.41, pred[2432]{0:T(1024)(128)(4,1)S(1)} %broadcast_in_dim.100), kind=kLoop, calls=%fused_computation.5.clone.1 | loop fusion | flops 11828032 | bytes 11841408 | tf_op jit(solution)/shard_map/while/body/eval_jaxpr/reduce_sum | solution.py:39
  117.6 2.6 %fusion.44 = f32[2,608,64]{1,2,0:T(8,128)S(1)} fusion(bf16[2432,2,64]{0,2,1:T(8,128)(2,1)S(1)} %bitcast.61, f32[2,2432,608]{1,2,0:T(8,128)S(1)} %get-tuple-element.191, f32[2,608]{1,0:T(2,128)S(1)} %fusion.41, pred[2432]{0:T(1024)(128)(4,1)S(1)} %broadcast_in_dim.100, f32[2,608,64]{1,2,0:T(8,128)S(1)} %copy-done.2, ...), kind=kOutput, calls=%fused_computation.8.clone.1 | convolution fusion | flops 390598656 | bytes 13086593 | tf_op jit(solution)/shard_map/while/body/eval_jaxpr/hqk,khd->hqd/dot_general | solution.py:40
  121.3 2.4 %constant_dynamic-slice_fusion.4 = (bf16[1,2432,128]{2,1,0:T(8,128)(2,1)}, bf16[1,2432,128]{2,1,0:T(8,128)(2,1)}) fusion(bf16[2,2432,128]{2,1,0:T(8,128)(2,1)} %get-tuple-element.222, s32[]{:T(128)S(6)} %copy.73, bf16[2,2432,128]{2,1,0:T(8,128)(2,1)} %get-tuple-element.220), kind=kLoop, calls=%fused_computation.16.clone.1 | loop fusion | bytes 2490372 | tf_op jit(solution)/shard_map/while/body/jit(dynamic_index_in_dim)/dynamic_slice | solution.py:70
  123.7 2.1 %copy.66 = bf16[1,2432,128]{1,2,0:T(8,128)(2,1)} copy(bf16[1,2432,128]{2,1,0:T(8,128)(2,1)} %get-tuple-element.189) | data formatting | bytes 1245184 | tf_op jit(solution)/shard_map/while/body/jit(dynamic_index_in_dim)/dynamic_slice | solution.py:70
  125.9 2.1 %copy.67 = bf16[1,2432,128]{1,2,0:T(8,128)(2,1)} copy(bf16[1,2432,128]{2,1,0:T(8,128)(2,1)} %get-tuple-element.193) | data formatting | bytes 1245184 | tf_op jit(solution)/shard_map/while/body/jit(dynamic_index_in_dim)/dynamic_slice | solution.py:70
  128.0 3.1 %bitcast_reduce_fusion.2 = (f32[2,608]{1,0:T(2,128)S(1)}, f32[2,2432,608]{1,2,0:T(8,128)S(1)}) fusion(pred[2432]{0:T(1024)(128)(4,1)S(1)} %broadcast_in_dim.100, bf16[2432,2,64]{0,2,1:T(8,128)(2,1)} %bitcast.60, bf16[608,2,64]{0,2,1:T(8,128)(2,1)S(1)} %get-tuple-element.221), kind=kOutput, calls=%fused_computation.1.clone.1 | convolution fusion | flops 387406656 | bytes 12614784 | tf_op jit(solution)/shard_map/while/body/eval_jaxpr/qhd,khd->hqk/dot_general | solution.py:32
  131.1 2.5 %fusion.42 = f32[2,608]{1,0:T(2,128)S(1)} fusion(f32[2,2432,608]{1,2,0:T(8,128)S(1)} %get-tuple-element.191, f32[2,608]{1,0:T(2,128)S(1)} %fusion.41, pred[2432]{0:T(1024)(128)(4,1)S(1)} %broadcast_in_dim.100), kind=kLoop, calls=%fused_computation.5.clone.1 | loop fusion | flops 11828032 | bytes 11841408 | tf_op jit(solution)/shard_map/while/body/eval_jaxpr/reduce_sum | solution.py:39
  133.7 2.6 %fusion.44 = f32[2,608,64]{1,2,0:T(8,128)S(1)} fusion(bf16[2432,2,64]{0,2,1:T(8,128)(2,1)S(1)} %bitcast.61, f32[2,2432,608]{1,2,0:T(8,128)S(1)} %get-tuple-element.191, f32[2,608]{1,0:T(2,128)S(1)} %fusion.41, pred[2432]{0:T(1024)(128)(4,1)S(1)} %broadcast_in_dim.100, f32[2,608,64]{1,2,0:T(8,128)S(1)} %copy-done.2, ...), kind=kOutput, calls=%fused_computation.8.clone.1 | convolution fusion | flops 390598656 | bytes 13086593 | tf_op jit(solution)/shard_map/while/body/eval_jaxpr/hqk,khd->hqd/dot_general | solution.py:40
  137.1 1.7 divide_convert_fusion
  140.7 4.6 %all-to-all-start.1 = ((bf16[4,2,9728]{2,1,0:T(2,128)(2,1)}), bf16[4,2,9728]{2,1,0:T(2,128)(2,1)}, u32[]{:S(2)}, u32[]{:S(2)}) async-start(bf16[4,2,9728]{2,1,0:T(2,128)(2,1)} %reshape.128), calls=%async_computation.1 | async-start | bytes 311296 | tf_op jit(solution)/shard_map/all_to_all | solution.py:115
  145.5 6.6 %all-to-all-done.1 = bf16[4,2,9728]{2,1,0:T(2,128)(2,1)} async-done(((bf16[4,2,9728]{2,1,0:T(2,128)(2,1)}), bf16[4,2,9728]{2,1,0:T(2,128)(2,1)}, u32[]{:S(2)}, u32[]{:S(2)}) %all-to-all-start.1) | async-done | bytes 155680 | tf_op jit(solution)/shard_map/all_to_all | solution.py:115
  155.4 2.5 %fusion.15 = bf16[152,1024]{1,0:T(8,128)(2,1)} fusion(f32[152,1024]{1,0:T(8,128)} %reshape.120, bf16[152,512]{1,0:T(8,128)(2,1)S(1)} %reshape.118, bf16[512,1024]{1,0:T(8,128)(2,1)} %param.13, pred[152]{0:T(512)(128)(4,1)S(1)} %broadcast_in_dim.59), kind=kOutput, calls=%fused_computation.25 | convolution fusion | flops 159850496 | bytes 2138264 | tf_op jit(solution)/shard_map/dot_general | solution.py:117
  (58 shorter events, 11.7 us)
Async XLA Ops:
  6.5 6.9 %copy-start = (bf16[1024,1536]{1,0:T(8,128)(2,1)S(1)}, bf16[1024,1536]{1,0:T(8,128)(2,1)}, u32[]{:S(2)}) copy-start(bf16[1024,1536]{1,0:T(8,128)(2,1)} %param.12) | copy-start | bytes 9437188
  6.5 50.4 %copy-start.4 = (u32[32]{0:T(128)S(1)}, u32[32]{0:T(128)}, u32[]{:S(2)}) copy-start(u32[32]{0:T(128)} %constant.36) | copy-start | bytes 388
  6.5 72.3 %all-gather.5.cloned.1.call-start = ((), (), s32[]{:S(2)}) async-start(), calls=%async_computation.3 | async-start | bytes 1400832 | tf_op jit(solution)/shard_map/all_gather | solution.py:107
  55.4 49.6 %all-gather.3.cloned.1.call-start = ((), (), s32[]{:S(2)}) async-start(), calls=%async_computation.2 | async-start | bytes 1400832 | tf_op jit(solution)/shard_map/all_gather | solution.py:106
  111.9 5.7 %copy-start.1 = (bf16[1,2432,128]{1,2,0:T(8,128)(2,1)S(1)}, bf16[1,2432,128]{1,2,0:T(8,128)(2,1)}, u32[]{:S(2)}) copy-start(bf16[1,2432,128]{1,2,0:T(8,128)(2,1)} %copy.67) | copy-start | bytes 1867780 | tf_op jit(solution)/shard_map/while
  111.9 5.7 %copy-start.2 = (f32[2,608,64]{1,2,0:T(8,128)S(1)}, f32[2,608,64]{1,2,0:T(8,128)}, u32[]{:S(2)}) copy-start(f32[2,608,64]{1,2,0:T(8,128)} %get-tuple-element.208) | copy-start | bytes 933892 | tf_op jit(solution)/shard_map/while
  120.3 0.7 copy-start.3
  128.0 5.7 %copy-start.1 = (bf16[1,2432,128]{1,2,0:T(8,128)(2,1)S(1)}, bf16[1,2432,128]{1,2,0:T(8,128)(2,1)}, u32[]{:S(2)}) copy-start(bf16[1,2432,128]{1,2,0:T(8,128)(2,1)} %copy.67) | copy-start | bytes 1867780 | tf_op jit(solution)/shard_map/while
  128.0 5.7 %copy-start.2 = (f32[2,608,64]{1,2,0:T(8,128)S(1)}, f32[2,608,64]{1,2,0:T(8,128)}, u32[]{:S(2)}) copy-start(f32[2,608,64]{1,2,0:T(8,128)} %get-tuple-element.208) | copy-start | bytes 933892 | tf_op jit(solution)/shard_map/while
  136.3 0.7 copy-start.3
  140.7 11.3 %all-to-all-start.1 = ((bf16[4,2,9728]{2,1,0:T(2,128)(2,1)}), bf16[4,2,9728]{2,1,0:T(2,128)(2,1)}, u32[]{:S(2)}, u32[]{:S(2)}) async-start(bf16[4,2,9728]{2,1,0:T(2,128)(2,1)} %reshape.128), calls=%async_computation.1 | async-start | bytes 311296 | tf_op jit(solution)/shard_map/all_to_all | solution.py:115
Sparse Core Ops, SparseCore 0:
  55.5 23.2 all-gather.4
  80.7 24.1 all-gather.2
where the time goes:
time: 168 us; the launch traced here: 167 us
  waiting for transfers between devices  45.1 us (27%)
  local copies, waits for them, and re-layouts  41.4 us (25%)
  blocking collectives  34.5 us (21%)
  matrix products  16.6 us (10%)
  between operations  14.8 us (9%)
  other arithmetic  9.53 us (6%)
  starting transfers between devices  4.64 us (3%)
    all_to_all x1, blocking collectives, on_device(): lax.all_to_all(stacked, 'frame', split_axis=2, concat_axis=0, tiled=True)  26.5 us
    all_gather x1, waiting for transfers between devices, on_device(): lax.all_gather(key_local, 'space', axis=0, tiled=True)  26.1 us
    dynamic_slice x6, local copies, waits for them, and re-layouts, fold_masked(): lax.scan(step_group, carry, (key_groups, value_groups, count_groups))  13.3 us
    all_gather x1, waiting for transfers between devices, on_device(): lax.all_gather(value_local, 'space', axis=0, tiled=True)  12.4 us
    unnamed x1, blocking collectives  8.09 us
    all_to_all x1, waiting for transfers between devices, on_device(): lax.all_to_all(attended, 'frame', split_axis=0, concat_axis=1, tiled=True)  6.57 us
    dot_general x2, matrix products, attend(): jnp.einsum('qhd,khd->hqk', query_heads, key_heads, preferred_element_type...  6.27 us
    dot_general x2, matrix products, attend(): jnp.einsum('hqk,khd->hqd', weights.astype(jnp.bfloat16), value_heads, pre...  5.28 us
  transfers between devices with their start and end apart: 3, of which 3 were waited for; matrix products, arithmetic and copies ran while one was open for 1% of the time, Pallas kernels for 0%

commit v1 on v0

--- a/solution.py
+++ b/solution.py
@@ -93,7 +93,12 @@
     frames = lax.axis_size("frame")
     local_heads = HEADS // frames
     stacked = projected.reshape(rows_dev, 3, HEADS, head_size)
-    regrouped = lax.all_to_all(stacked, "frame", split_axis=2, concat_axis=0, tiled=True)
+    regrouped = jnp.concatenate(
+        lax.all_to_all(
+            jnp.stack(jnp.split(stacked, lax.axis_size("frame"), axis=2)), "frame", 0, 0
+        ),
+        axis=0,
+    )
     all_rows = regrouped.shape[0]
     query_local = regrouped[:, 0]
     key_local = regrouped[:, 1].reshape(all_rows, local_heads * head_size)

time: 168 us -> 174 us (1.036)
  local copies, waits for them, and re-layouts: 41.4 us -> 45 us
  other arithmetic: 9.53 us -> 12.3 us
    another operation x0 -> x2, local copies, waits for them, and re-layouts: none -> 6.34 us  [on_device(): jnp.stack(jnp.split(stacked, lax.axis_size('frame'), axis=2))]
    reshape x2 -> x1, local copies, waits for them, and re-layouts: 5.19 us -> 2.39 us  [on_device(): stacked = projected.reshape(rows_dev, 3, HEADS, head_size)]
    another operation x0 -> x1, other arithmetic: none -> 2.72 us  [on_device(): jnp.stack(jnp.split(stacked, lax.axis_size('frame'), axis=2))]
    all_to_all x2 -> x1, local copies, waits for them, and re-layouts: 4.17 us -> 1.5 us  [on_device(): lax.all_to_all(jnp.stack(jnp.split(stacked, lax.axis_size('frame'), axis=...]
    reshape x0 -> x1, local copies, waits for them, and re-layouts: none -> 2.67 us  [on_device(): jnp.concatenate(lax.all_to_all(jnp.stack(jnp.split(stacked, lax.axis_size...]
where the time goes in v1:
time: 174 us; the launch traced here: 173 us
  waiting for transfers between devices  45.1 us (26%)
  local copies, waits for them, and re-layouts  45 us (26%)
  blocking collectives  34.5 us (20%)
  matrix products  16.6 us (10%)
  between operations  14.8 us (9%)
  other arithmetic  12.3 us (7%)
  starting transfers between devices  4.64 us (3%)
    all_to_all x1, blocking collectives, on_device(): lax.all_to_all(jnp.stack(jnp.split(stacked, lax.axis_size('frame'), axis=...  26.5 us
    all_gather x1, waiting for transfers between devices, on_device(): lax.all_gather(key_local, 'space', axis=0, tiled=True)  26.1 us
    dynamic_slice x6, local copies, waits for them, and re-layouts, fold_masked(): lax.scan(step_group, carry, (key_groups, value_groups, count_groups))  13.4 us
    all_gather x1, waiting for transfers between devices, on_device(): lax.all_gather(value_local, 'space', axis=0, tiled=True)  12.4 us
    unnamed x1, blocking collectives  8.08 us
    all_to_all x1, waiting for transfers between devices, on_device(): lax.all_to_all(attended, 'frame', split_axis=0, concat_axis=1, tiled=True)  6.57 us
    another operation x2, local copies, waits for them, and re-layouts, on_device(): jnp.stack(jnp.split(stacked, lax.axis_size('frame'), axis=2))  6.34 us
    dot_general x2, matrix products, attend(): jnp.einsum('qhd,khd->hqk', query_heads, key_heads, preferred_element_type...  6.26 us
  transfers between devices with their start and end apart: 3, of which 3 were waited for; matrix products, arithmetic and copies ran while one was open for 1% of the time, Pallas kernels for 0%

profile of v1, /device:TPU:0, one launch (start us, length us, event | category | flops | bytes accessed | tf_op | source)
XLA Modules:
  0.0 173.1 jit_solution(9026521304486175056)
XLA Ops:
  9.3 1.9 %copy.55 = f32[4,38,1024]{2,1,0:T(8,128)} copy(bf16[4,38,1024]{2,0,1:T(4,128)(2,1)} %param.8) | data formatting | bytes 933888 | tf_op jit(solution)/shard_map/convert_element_type | solution.py:122
  11.4 2.0 %reshape.124 = f32[152,1024]{1,0:T(8,128)} reshape(f32[4,38,1024]{2,1,0:T(8,128)} %copy.55) | data formatting | bytes 1245184 | tf_op jit(solution)/shard_map/convert_element_type | solution.py:122
  13.4 2.6 %convolution_convert_fusion = bf16[152,1536]{1,0:T(8,128)(2,1)} fusion(bf16[1024,1536]{1,0:T(8,128)(2,1)S(1)} %copy-done, f32[152,1024]{1,0:T(8,128)} %reshape.124, f32[1024]{0:T(1024)} %param.11, f32[1024]{0:T(1024)} %param.10, f32[152]{0:T(256)S(1)} %rsqrt.12, f32[152]{0:T(256)S(1)} %div.17), kind=kOutput, calls=%fused_computation.22 | convolution fusion | flops 479162368 | bytes 4244672 | tf_op jit(solution)/shard_map/dot_general | solution.py:91
  16.1 2.4 %reshape.118 = bf16[152,3,8,64]{3,2,1,0:T(8,128)(2,1)} reshape(bf16[152,1536]{1,0:T(8,128)(2,1)} %convolution_convert_fusion) | data formatting | bytes 933888 | tf_op jit(solution)/shard_map/reshape | solution.py:95
  18.5 3.2 %slice_bitcast_fusion.3 = (bf16[1,152,3,2,64]{4,3,2,1,0:T(2,128)(2,1)S(1)}, bf16[1,152,3,2,64]{4,3,2,1,0:T(2,128)(2,1)S(1)}, bf16[1,152,3,2,64]{4,3,2,1,0:T(2,128)(2,1)S(1)}, bf16[1,152,3,2,64]{4,3,2,1,0:T(2,128)(2,1)S(1)}) fusion(bf16[152,3,8,64]{3,2,1,0:T(8,128)(2,1)} %reshape.118), kind=kLoop, calls=%fused_computation.39 | loop fusion | bytes 933888 | tf_op jit(solution)/shard_map/stack | solution.py:98
  21.7 2.7 %pad_maximum_fusion = bf16[4,152,3,2,64]{4,3,2,1,0:T(2,128)(2,1)} fusion(bf16[1,152,3,2,64]{4,3,2,1,0:T(2,128)(2,1)S(1)} %get-tuple-element.140, bf16[1,152,3,2,64]{4,3,2,1,0:T(2,128)(2,1)S(1)} %get-tuple-element.141, bf16[1,152,3,2,64]{4,3,2,1,0:T(2,128)(2,1)S(1)} %get-tuple-element.142, bf16[1,152,3,2,64]{4,3,2,1,0:T(2,128)(2,1)S(1)} %get-tuple-element.139), kind=kLoop, calls=%fused_computation.26 | loop fusion | flops 700416 | bytes 933888 | tf_op jit(solution)/shard_map/stack | solution.py:98
  24.4 3.1 %copy.59 = bf16[4,152,3,2,64]{1,4,3,2,0:T(8,128)(2,1)} copy(bf16[4,152,3,2,64]{4,3,2,1,0:T(2,128)(2,1)} %pad_maximum_fusion) | data formatting | bytes 933888 | tf_op jit(solution)/shard_map/stack | solution.py:98
  27.5 26.5 %all_to_all.20 = bf16[4,152,3,2,64]{1,4,3,2,0:T(8,128)(2,1)S(1)} all-to-all(bf16[4,152,3,2,64]{1,4,3,2,0:T(8,128)(2,1)} %copy.59), channel_id=1, replica_groups=mesh['frame'=4,'space'=8] {'frame'}, dimensions={0} | all-to-all | bytes 933888 | tf_op jit(solution)/shard_map/all_to_all | solution.py:97
  54.0 1.5 copy.60
  55.5 2.7 %reshape.119 = bf16[608,3,2,64]{0,3,2,1:T(8,128)(2,1)} reshape(bf16[4,152,3,2,64]{1,0,4,3,2:T(4,128)(2,1)} %copy.60) | data formatting | bytes 933888 | tf_op jit(solution)/shard_map/reshape | solution.py:96
  58.2 1.8 %fusion.20 = (bf16[608,1,2,64]{0,3,2,1:T(8,128)(2,1)}, bf16[608,2,64]{0,2,1:T(8,128)(2,1)S(1)}, bf16[608,1,2,64]{0,3,2,1:T(8,128)(2,1)S(1)}) fusion(bf16[608,3,2,64]{0,3,2,1:T(8,128)(2,1)} %reshape.119), kind=kLoop, calls=%fused_computation.45 | loop fusion | bytes 933888 | tf_op jit(solution)/shard_map/slice | solution.py:105
  59.9 1.7 copy.62
  64.5 8.1 %all-reduce = s32[32]{0:T(128)S(1)} all-reduce(s32[32]{0:T(128)S(1)} %broadcast_dynamic-update-slice_fusion), channel_id=1, replica_groups=mesh['frame'=4,'space'=8] {'space'}, use_global_device_ids=true, to_apply=%add | all-reduce | flops 32 | bytes 256
  72.7 12.4 %all-gather.5.cloned.1.call-done = bf16[4864,128]{1,0:T(8,128)(2,1)} async-done(((bf16[608,128]{1,0:T(8,128)(2,1)}), bf16[4864,128]{1,0:T(8,128)(2,1)}) %all-gather.5.cloned.1.call-update) | async-done | bytes 1245200 | tf_op jit(solution)/shard_map/all_gather | solution.py:112
  85.1 26.1 %all-gather.3.cloned.1.call-done = bf16[4864,128]{1,0:T(8,128)(2,1)} async-done(((bf16[608,128]{1,0:T(8,128)(2,1)}), bf16[4864,128]{1,0:T(8,128)(2,1)}) %all-gather.3.cloned.1.call-update) | async-done | bytes 1245200 | tf_op jit(solution)/shard_map/all_gather | solution.py:111
  111.2 32.2 %while.15 = (s32[]{:T(128)}, f32[2,608]{1,0:T(2,128)S(1)}, f32[2,608]{1,0:T(2,128)S(1)}, f32[2,608,64]{1,2,0:T(8,128)}, s32[2,16]{1,0:T(2,128)S(1)}, /*index=5*/...) while((s32[]{:T(128)}, f32[2,608]{1,0:T(2,128)S(1)}, ...), condition=%wide.region_5.6_spmd.clone, body=%wide.region_2.5_spmd.clone.sunk | while | flops 789841920 | bytes 47565588 | solution.py:70
  111.6 2.4 %constant_dynamic-slice_fusion.4 = (bf16[1,2432,128]{2,1,0:T(8,128)(2,1)}, bf16[1,2432,128]{2,1,0:T(8,128)(2,1)}) fusion(bf16[2,2432,128]{2,1,0:T(8,128)(2,1)} %get-tuple-element.234, s32[]{:T(128)S(6)} %copy.86, bf16[2,2432,128]{2,1,0:T(8,128)(2,1)} %get-tuple-element.232), kind=kLoop, calls=%fused_computation.16.clone.1 | loop fusion | bytes 2490372 | tf_op jit(solution)/shard_map/while/body/jit(dynamic_index_in_dim)/dynamic_slice | solution.py:70
  114.0 2.1 %copy.79 = bf16[1,2432,128]{1,2,0:T(8,128)(2,1)} copy(bf16[1,2432,128]{2,1,0:T(8,128)(2,1)} %get-tuple-element.201) | data formatting | bytes 1245184 | tf_op jit(solution)/shard_map/while/body/jit(dynamic_index_in_dim)/dynamic_slice | solution.py:70
  116.1 2.2 %copy.80 = bf16[1,2432,128]{1,2,0:T(8,128)(2,1)} copy(bf16[1,2432,128]{2,1,0:T(8,128)(2,1)} %get-tuple-element.205) | data formatting | bytes 1245184 | tf_op jit(solution)/shard_map/while/body/jit(dynamic_index_in_dim)/dynamic_slice | solution.py:70
  118.2 3.1 %bitcast_reduce_fusion.2 = (f32[2,608]{1,0:T(2,128)S(1)}, f32[2,2432,608]{1,2,0:T(8,128)S(1)}) fusion(pred[2432]{0:T(1024)(128)(4,1)S(1)} %broadcast_in_dim.100, bf16[2432,2,64]{0,2,1:T(8,128)(2,1)} %bitcast.65, bf16[608,2,64]{0,2,1:T(8,128)(2,1)S(1)} %get-tuple-element.233), kind=kOutput, calls=%fused_computation.1.clone.1 | convolution fusion | flops 387406656 | bytes 12614784 | tf_op jit(solution)/shard_map/while/body/eval_jaxpr/qhd,khd->hqk/dot_general | solution.py:32
  121.4 2.5 %fusion.42 = f32[2,608]{1,0:T(2,128)S(1)} fusion(f32[2,2432,608]{1,2,0:T(8,128)S(1)} %get-tuple-element.203, f32[2,608]{1,0:T(2,128)S(1)} %fusion.41, pred[2432]{0:T(1024)(128)(4,1)S(1)} %broadcast_in_dim.100), kind=kLoop, calls=%fused_computation.5.clone.1 | loop fusion | flops 11828032 | bytes 11841408 | tf_op jit(solution)/shard_map/while/body/eval_jaxpr/reduce_sum | solution.py:39
  123.9 2.6 %fusion.44 = f32[2,608,64]{1,2,0:T(8,128)S(1)} fusion(bf16[2432,2,64]{0,2,1:T(8,128)(2,1)S(1)} %bitcast.66, f32[2,2432,608]{1,2,0:T(8,128)S(1)} %get-tuple-element.203, f32[2,608]{1,0:T(2,128)S(1)} %fusion.41, pred[2432]{0:T(1024)(128)(4,1)S(1)} %broadcast_in_dim.100, f32[2,608,64]{1,2,0:T(8,128)S(1)} %copy-done.2, ...), kind=kOutput, calls=%fused_computation.8.clone.1 | convolution fusion | flops 390598656 | bytes 13086593 | tf_op jit(solution)/shard_map/while/body/eval_jaxpr/hqk,khd->hqd/dot_general | solution.py:40
  127.7 2.4 %constant_dynamic-slice_fusion.4 = (bf16[1,2432,128]{2,1,0:T(8,128)(2,1)}, bf16[1,2432,128]{2,1,0:T(8,128)(2,1)}) fusion(bf16[2,2432,128]{2,1,0:T(8,128)(2,1)} %get-tuple-element.234, s32[]{:T(128)S(6)} %copy.86, bf16[2,2432,128]{2,1,0:T(8,128)(2,1)} %get-tuple-element.232), kind=kLoop, calls=%fused_computation.16.clone.1 | loop fusion | bytes 2490372 | tf_op jit(solution)/shard_map/while/body/jit(dynamic_index_in_dim)/dynamic_slice | solution.py:70
  130.0 2.1 %copy.79 = bf16[1,2432,128]{1,2,0:T(8,128)(2,1)} copy(bf16[1,2432,128]{2,1,0:T(8,128)(2,1)} %get-tuple-element.201) | data formatting | bytes 1245184 | tf_op jit(solution)/shard_map/while/body/jit(dynamic_index_in_dim)/dynamic_slice | solution.py:70
  132.2 2.2 %copy.80 = bf16[1,2432,128]{1,2,0:T(8,128)(2,1)} copy(bf16[1,2432,128]{2,1,0:T(8,128)(2,1)} %get-tuple-element.205) | data formatting | bytes 1245184 | tf_op jit(solution)/shard_map/while/body/jit(dynamic_index_in_dim)/dynamic_slice | solution.py:70
  134.3 3.1 %bitcast_reduce_fusion.2 = (f32[2,608]{1,0:T(2,128)S(1)}, f32[2,2432,608]{1,2,0:T(8,128)S(1)}) fusion(pred[2432]{0:T(1024)(128)(4,1)S(1)} %broadcast_in_dim.100, bf16[2432,2,64]{0,2,1:T(8,128)(2,1)} %bitcast.65, bf16[608,2,64]{0,2,1:T(8,128)(2,1)S(1)} %get-tuple-element.233), kind=kOutput, calls=%fused_computation.1.clone.1 | convolution fusion | flops 387406656 | bytes 12614784 | tf_op jit(solution)/shard_map/while/body/eval_jaxpr/qhd,khd->hqk/dot_general | solution.py:32
  137.5 2.5 %fusion.42 = f32[2,608]{1,0:T(2,128)S(1)} fusion(f32[2,2432,608]{1,2,0:T(8,128)S(1)} %get-tuple-element.203, f32[2,608]{1,0:T(2,128)S(1)} %fusion.41, pred[2432]{0:T(1024)(128)(4,1)S(1)} %broadcast_in_dim.100), kind=kLoop, calls=%fused_computation.5.clone.1 | loop fusion | flops 11828032 | bytes 11841408 | tf_op jit(solution)/shard_map/while/body/eval_jaxpr/reduce_sum | solution.py:39
  140.0 2.6 %fusion.44 = f32[2,608,64]{1,2,0:T(8,128)S(1)} fusion(bf16[2432,2,64]{0,2,1:T(8,128)(2,1)S(1)} %bitcast.66, f32[2,2432,608]{1,2,0:T(8,128)S(1)} %get-tuple-element.203, f32[2,608]{1,0:T(2,128)S(1)} %fusion.41, pred[2432]{0:T(1024)(128)(4,1)S(1)} %broadcast_in_dim.100, f32[2,608,64]{1,2,0:T(8,128)S(1)} %copy-done.2, ...), kind=kOutput, calls=%fused_computation.8.clone.1 | convolution fusion | flops 390598656 | bytes 13086593 | tf_op jit(solution)/shard_map/while/body/eval_jaxpr/hqk,khd->hqd/dot_general | solution.py:40
  143.4 1.7 divide_convert_fusion
  147.1 4.6 %all-to-all-start.1 = ((bf16[4,2,9728]{2,1,0:T(2,128)(2,1)}), bf16[4,2,9728]{2,1,0:T(2,128)(2,1)}, u32[]{:S(2)}, u32[]{:S(2)}) async-start(bf16[4,2,9728]{2,1,0:T(2,128)(2,1)} %reshape.132), calls=%async_computation.1 | async-start | bytes 311296 | tf_op jit(solution)/shard_map/all_to_all | solution.py:120
  151.8 6.6 %all-to-all-done.1 = bf16[4,2,9728]{2,1,0:T(2,128)(2,1)} async-done(((bf16[4,2,9728]{2,1,0:T(2,128)(2,1)}), bf16[4,2,9728]{2,1,0:T(2,128)(2,1)}, u32[]{:S(2)}, u32[]{:S(2)}) %all-to-all-start.1) | async-done | bytes 155680 | tf_op jit(solution)/shard_map/all_to_all | solution.py:120
  161.7 2.5 %fusion.15 = bf16[152,1024]{1,0:T(8,128)(2,1)} fusion(f32[152,1024]{1,0:T(8,128)} %reshape.124, bf16[152,512]{1,0:T(8,128)(2,1)S(1)} %reshape.122, bf16[512,1024]{1,0:T(8,128)(2,1)} %param.13, pred[152]{0:T(512)(128)(4,1)S(1)} %broadcast_in_dim.59), kind=kOutput, calls=%fused_computation.25 | convolution fusion | flops 159850496 | bytes 2138264 | tf_op jit(solution)/shard_map/dot_general | solution.py:122
  (60 shorter events, 14.2 us)
Async XLA Ops:
  6.5 6.9 %copy-start = (bf16[1024,1536]{1,0:T(8,128)(2,1)S(1)}, bf16[1024,1536]{1,0:T(8,128)(2,1)}, u32[]{:S(2)}) copy-start(bf16[1024,1536]{1,0:T(8,128)(2,1)} %param.12) | copy-start | bytes 9437188
  6.5 56.7 %copy-start.4 = (u32[32]{0:T(128)S(1)}, u32[32]{0:T(128)}, u32[]{:S(2)}) copy-start(u32[32]{0:T(128)} %constant.36) | copy-start | bytes 388
  6.5 78.6 %all-gather.5.cloned.1.call-start = ((), (), s32[]{:S(2)}) async-start(), calls=%async_computation.3 | async-start | bytes 1400832 | tf_op jit(solution)/shard_map/all_gather | solution.py:112
  61.7 49.6 %all-gather.3.cloned.1.call-start = ((), (), s32[]{:S(2)}) async-start(), calls=%async_computation.2 | async-start | bytes 1400832 | tf_op jit(solution)/shard_map/all_gather | solution.py:111
  118.2 5.7 %copy-start.1 = (bf16[1,2432,128]{1,2,0:T(8,128)(2,1)S(1)}, bf16[1,2432,128]{1,2,0:T(8,128)(2,1)}, u32[]{:S(2)}) copy-start(bf16[1,2432,128]{1,2,0:T(8,128)(2,1)} %copy.80) | copy-start | bytes 1867780 | tf_op jit(solution)/shard_map/while
  118.2 5.7 %copy-start.2 = (f32[2,608,64]{1,2,0:T(8,128)S(1)}, f32[2,608,64]{1,2,0:T(8,128)}, u32[]{:S(2)}) copy-start(f32[2,608,64]{1,2,0:T(8,128)} %get-tuple-element.220) | copy-start | bytes 933892 | tf_op jit(solution)/shard_map/while
  126.6 0.7 copy-start.3
  134.3 5.7 %copy-start.1 = (bf16[1,2432,128]{1,2,0:T(8,128)(2,1)S(1)}, bf16[1,2432,128]{1,2,0:T(8,128)(2,1)}, u32[]{:S(2)}) copy-start(bf16[1,2432,128]{1,2,0:T(8,128)(2,1)} %copy.80) | copy-start | bytes 1867780 | tf_op jit(solution)/shard_map/while
  134.3 5.7 %copy-start.2 = (f32[2,608,64]{1,2,0:T(8,128)S(1)}, f32[2,608,64]{1,2,0:T(8,128)}, u32[]{:S(2)}) copy-start(f32[2,608,64]{1,2,0:T(8,128)} %get-tuple-element.220) | copy-start | bytes 933892 | tf_op jit(solution)/shard_map/while
  142.7 0.7 copy-start.3
  147.1 11.3 %all-to-all-start.1 = ((bf16[4,2,9728]{2,1,0:T(2,128)(2,1)}), bf16[4,2,9728]{2,1,0:T(2,128)(2,1)}, u32[]{:S(2)}, u32[]{:S(2)}) async-start(bf16[4,2,9728]{2,1,0:T(2,128)(2,1)} %reshape.132), calls=%async_computation.1 | async-start | bytes 311296 | tf_op jit(solution)/shard_map/all_to_all | solution.py:120
Sparse Core Ops, SparseCore 0:
  61.8 23.2 all-gather.4
  87.0 24.1 all-gather.2
